TPU v7x, 32 devices: a whole 2x2x4 slice. The times are simulated.
32 devices in a mesh: groups: 2 (over y), tm: 4 (over z), chan: 4 (over x, core).
Axes of the slice: x: 2, y: 2, z: 4, core: 2. Of those that a mesh axis runs over, the one named last changes fastest.
Arguments:
- vis: bfloat16 [8, 128, 2, 128], P(('groups', 'chan'), 'tm'), parts along dimension 0, may hold values from -6 to 6
- row_weight: bfloat16 [8, 128, 128, 128], P(('groups', 'chan'), 'tm'), parts along dimension 0, may hold values from -4 to 4
- col_weight: bfloat16 [8, 128, 128, 256], P(('groups', 'chan'), 'tm'), parts along dimension 0, may hold values from -0.5 to 0.5
- w_bin: int32 [8, 128, 1], P(('groups', 'chan'), 'tm'), parts along dimension 0, may hold values from 0 to 3; in each aligned block of 32 rows (0 to 31, 32 to 63, ..., all dimensions but the last counted through in order) at most 16 rows name the same one
- tile_col: int32 [8, 128], P(('groups', 'chan'), 'tm'), parts along dimension 0, may hold values from 0 to 15
- w_kernel: bfloat16 [8, 512, 512], P(('groups', 'tm')), parts along dimension 0, may hold values from -0.25 to 0.25
Outputs:
- grid: float32 [8, 128, 16, 512], P(('groups', 'tm'), 'chan'), parts along dimension 0
There are 2 independent parts, one for each index of `groups`. A program takes and returns all parts, laid end to end along the dimension named above; each array names one. Nothing has to cross between parts.
Inputs may be any that keep to these rules, and one draw needn't show every extreme that they name: `w_bin`: within the blocks of one device (aligned blocks of 32 along the channel-group and block dimensions taken together), no w-plane is named more than 16 times, a bound that some block reaches.
All inputs are finite; a program needn't handle non-finite values.
Results may differ from a plain program's by a relative error of at most 0.0041.
Values may be sent and summed in bfloat16 or wider, within the bound.
A program may use at most 128 MiB of HBM per device.

v0:
```python
import jax
import jax.numpy as jnp
from jax import lax
from jax.sharding import PartitionSpec as P

QW = 256
GC = 4096


def grid_group(total, weighted, columns, targets):
    patch = jnp.einsum("ghkv,gvq->gkhq", weighted, columns, preferred_element_type=jnp.float32)
    flat = patch.reshape(patch.shape[0], -1)
    return total.at[targets].add(flat, mode="drop")


def weigh_rows(rows, visibility):
    return (
        rows.astype(jnp.float32)[:, None, :, :] * visibility.astype(jnp.float32)[:, :, None, :]
    ).astype(jnp.bfloat16)


def body(vis, row_weight, col_weight, w_bin, tile_col, w_kernel):
    planes = lax.axis_size("tm")
    count = vis.shape[1]
    rows_k = row_weight.shape[2]
    width_v = vis.shape[3]
    width_q = col_weight.shape[3]
    tile_count = GC // QW
    per_plane = 2 * count // planes
    slot_total = planes * per_plane
    turns = 4
    group_len = slot_total // turns
    bins = w_bin[0, :, 0]
    tiles = tile_col[0]
    member = (bins[:, None] == jnp.arange(planes, dtype=jnp.int32)[None, :]).astype(jnp.int32)
    before = jnp.cumsum(member, axis=0) - member
    within = jnp.sum(before * member, axis=1)
    target = bins * per_plane + within
    source = (
        jnp.full((slot_total,), count, jnp.int32).at[target].set(jnp.arange(count, dtype=jnp.int32))
    )
    filled = source < count
    picked = jnp.minimum(source, count - 1)
    slot_tile = jnp.where(filled, tiles[picked], tile_count).reshape(planes, per_plane)
    columns = jnp.take(col_weight[0], picked, axis=0).reshape(planes, per_plane, width_v, width_q)
    start = jnp.zeros((tile_count, rows_k * 2 * width_q), jnp.float32)
    rows_sent = jnp.take(row_weight[0], picked, axis=0).reshape(planes, per_plane, rows_k, width_v)
    vis_sent = jnp.take(vis[0], picked, axis=0).reshape(planes, per_plane, 2, width_v)
    got_rows, got_vis, got_columns, got_tiles = (
        lax.all_to_all(rows_sent, "tm", split_axis=0, concat_axis=0, tiled=True),
        lax.all_to_all(vis_sent, "tm", split_axis=0, concat_axis=0, tiled=True),
        lax.all_to_all(columns, "tm", split_axis=0, concat_axis=0, tiled=True),
        lax.all_to_all(slot_tile, "tm", split_axis=0, concat_axis=0, tiled=True),
    )

    def step_raw(total, group):
        rows, visibility, cols, targets = group
        return (grid_group(total, weigh_rows(rows, visibility), cols, targets), None)

    groups = (
        got_rows.reshape(turns, group_len, rows_k, width_v),
        got_vis.reshape(turns, group_len, 2, width_v),
        got_columns.reshape(turns, group_len, width_v, width_q),
        got_tiles.reshape(turns, group_len),
    )
    total, _ = lax.scan(step_raw, start, groups)
    partial_value = total.reshape(tile_count, rows_k, 2 * width_q)
    share = rows_k // lax.axis_size("chan")
    summed = lax.psum(partial_value, "chan")
    mine = lax.dynamic_slice_in_dim(summed, lax.axis_index("chan") * share, share, 1)
    rounded = mine.astype(jnp.bfloat16)
    result = jnp.einsum("tkq,qr->ktr", rounded, w_kernel[0], preferred_element_type=jnp.float32)
    return result[None]


def solution(mesh):
    in_specs = (
        P(("groups", "chan"), "tm", None, None),
        P(("groups", "chan"), "tm", None, None),
        P(("groups", "chan"), "tm", None, None),
        P(("groups", "chan"), "tm", None),
        P(("groups", "chan"), "tm"),
        P(("groups", "tm"), None, None),
    )
    out_specs = P(("groups", "tm"), "chan", None, None)
    return jax.shard_map(body, mesh=mesh, in_specs=in_specs, out_specs=out_specs, check_vma=False)
```

profile of v0, /device:TPU:1, one launch (start us, length us, event | category | flops | bytes accessed | tf_op | source)
XLA Modules:
  0.0 493.3 jit_solution(4983551968529737838)
XLA Ops:
  5.3 5.4 %all-to-all-start = ((s32[4,1,16]{2,1,0:T(1,128)}), s32[4,1,16]{2,1,0:T(1,128)S(1)}, u32[]{:S(2)}, u32[]{:S(2)}) async-start(s32[4,1,16]{2,1,0:T(1,128)} %bitcast.13), calls=%async_computation | async-start | bytes 4096 | tf_op jit(solution)/shard_map/all_to_all | solution.py:53
  16.3 4.5 all-to-all-start.3
  25.3 4.4 all-to-all-start.2
  32.6 6.4 %copy.14 = bf16[64,128,256]{1,2,0:T(8,128)(2,1)} copy(bf16[64,128,256]{2,1,0:T(8,128)(2,1)} %gather_fusion.1) | data formatting | bytes 8388608 | tf_op jit(solution)/shard_map/jit(_take)/gather | solution.py:45
  39.0 4.6 broadcast_select_fusion
  43.6 34.0 %all-to-all-done.2 = bf16[4,16,128,128]{3,2,1,0:T(8,128)(2,1)} async-done(((bf16[4,16,128,128]{3,2,1,0:T(8,128)(2,1)}), bf16[4,16,128,128]{3,2,1,0:T(8,128)(2,1)}, u32[]{:S(2)}, u32[]{:S(2)}) %all-to-all-start.2) | async-done | bytes 2097184 | tf_op jit(solution)/shard_map/all_to_all | solution.py:50
  77.6 5.0 %all-to-all-start.1 = ((bf16[4,16,128,256]{2,3,1,0:T(8,128)(2,1)}), bf16[4,16,128,256]{2,3,1,0:T(8,128)(2,1)}, u32[]{:S(2)}, u32[]{:S(2)}) async-start(bf16[4,16,128,256]{2,3,1,0:T(8,128)(2,1)} %broadcast_select_fusion), calls=%async_computation.1 | async-start | bytes 8388608 | tf_op jit(solution)/shard_map/all_to_all | solution.py:52
  82.6 92.6 %all-to-all-done.1 = bf16[4,16,128,256]{2,3,1,0:T(8,128)(2,1)} async-done(((bf16[4,16,128,256]{2,3,1,0:T(8,128)(2,1)}), bf16[4,16,128,256]{2,3,1,0:T(8,128)(2,1)}, u32[]{:S(2)}, u32[]{:S(2)}) %all-to-all-start.1) | async-done | bytes 4194336 | tf_op jit(solution)/shard_map/all_to_all | solution.py:52
  177.5 227.6 %while.10 = (s32[]{:T(128)}, f32[16,65536]{1,0:T(8,128)}, s32[4,16]{1,0:T(4,128)S(1)}, bf16[4,16,128,256]{2,3,1,0:T(8,128)(2,1)}, bf16[4,16,128,128]{3,2,1,0:T(8...) while((s32[]{:T(128)}, f32[16,65536]{1,0:T(8,128)}, s32[4,16]{1,0:T(4,128)S(1)}, ...), condition=%wide.region_5.6_spmd, body=%wide.region_3.5_spmd.sunk | while | flops 270798912 | bytes 37266200 | solution.py:66
  178.6 3.9 convolution_bitcast_fusion.3
  182.5 7.2 %copy.19 = f32[16,128,2,256]{3,2,1,0:T(2,128)} copy(f32[16,128,2,256]{1,3,2,0:T(8,128)} %convolution_bitcast_fusion.3) | data formatting | bytes 8388608 | tf_op jit(solution)/shard_map/while/body/eval_jaxpr/ghkv,gvq->gkhq/transpose | solution.py:11
  189.7 6.3 %reshape.160 = f32[16,65536]{1,0:T(8,128)} reshape(f32[16,128,2,256]{3,2,1,0:T(2,128)} %copy.19) | data formatting | bytes 8388608 | tf_op jit(solution)/shard_map/while/body/eval_jaxpr/reshape | solution.py:12
  196.1 38.3 %scatter_fusion = f32[16,65536]{1,0:T(8,128)} fusion(f32[16,65536]{1,0:T(8,128)} %get-tuple-element.97, s32[16]{0:T(128)S(1)} %fusion.16, f32[16,65536]{1,0:T(8,128)} %reshape.160), kind=kCustom, calls=%fused_computation.4.clone.1 | custom fusion | flops 1048576 | bytes 12582976 | tf_op jit(solution)/shard_map/while/body/eval_jaxpr/scatter-add | solution.py:13
  239.5 7.2 %copy.19 = f32[16,128,2,256]{3,2,1,0:T(2,128)} copy(f32[16,128,2,256]{1,3,2,0:T(8,128)} %convolution_bitcast_fusion.3) | data formatting | bytes 8388608 | tf_op jit(solution)/shard_map/while/body/eval_jaxpr/ghkv,gvq->gkhq/transpose | solution.py:11
  246.7 6.3 %reshape.160 = f32[16,65536]{1,0:T(8,128)} reshape(f32[16,128,2,256]{3,2,1,0:T(2,128)} %copy.19) | data formatting | bytes 8388608 | tf_op jit(solution)/shard_map/while/body/eval_jaxpr/reshape | solution.py:12
  253.0 38.0 %scatter_fusion = f32[16,65536]{1,0:T(8,128)} fusion(f32[16,65536]{1,0:T(8,128)} %get-tuple-element.97, s32[16]{0:T(128)S(1)} %fusion.16, f32[16,65536]{1,0:T(8,128)} %reshape.160), kind=kCustom, calls=%fused_computation.4.clone.1 | custom fusion | flops 1048576 | bytes 12582976 | tf_op jit(solution)/shard_map/while/body/eval_jaxpr/scatter-add | solution.py:13
  296.0 7.2 %copy.19 = f32[16,128,2,256]{3,2,1,0:T(2,128)} copy(f32[16,128,2,256]{1,3,2,0:T(8,128)} %convolution_bitcast_fusion.3) | data formatting | bytes 8388608 | tf_op jit(solution)/shard_map/while/body/eval_jaxpr/ghkv,gvq->gkhq/transpose | solution.py:11
  303.2 6.3 %reshape.160 = f32[16,65536]{1,0:T(8,128)} reshape(f32[16,128,2,256]{3,2,1,0:T(2,128)} %copy.19) | data formatting | bytes 8388608 | tf_op jit(solution)/shard_map/while/body/eval_jaxpr/reshape | solution.py:12
  309.6 38.6 %scatter_fusion = f32[16,65536]{1,0:T(8,128)} fusion(f32[16,65536]{1,0:T(8,128)} %get-tuple-element.97, s32[16]{0:T(128)S(1)} %fusion.16, f32[16,65536]{1,0:T(8,128)} %reshape.160), kind=kCustom, calls=%fused_computation.4.clone.1 | custom fusion | flops 1048576 | bytes 12582976 | tf_op jit(solution)/shard_map/while/body/eval_jaxpr/scatter-add | solution.py:13
  353.2 7.2 %copy.19 = f32[16,128,2,256]{3,2,1,0:T(2,128)} copy(f32[16,128,2,256]{1,3,2,0:T(8,128)} %convolution_bitcast_fusion.3) | data formatting | bytes 8388608 | tf_op jit(solution)/shard_map/while/body/eval_jaxpr/ghkv,gvq->gkhq/transpose | solution.py:11
  360.4 6.3 %reshape.160 = f32[16,65536]{1,0:T(8,128)} reshape(f32[16,128,2,256]{3,2,1,0:T(2,128)} %copy.19) | data formatting | bytes 8388608 | tf_op jit(solution)/shard_map/while/body/eval_jaxpr/reshape | solution.py:12
  366.8 38.3 %scatter_fusion = f32[16,65536]{1,0:T(8,128)} fusion(f32[16,65536]{1,0:T(8,128)} %get-tuple-element.97, s32[16]{0:T(128)S(1)} %fusion.16, f32[16,65536]{1,0:T(8,128)} %reshape.160), kind=kCustom, calls=%fused_computation.4.clone.1 | custom fusion | flops 1048576 | bytes 12582976 | tf_op jit(solution)/shard_map/while/body/eval_jaxpr/scatter-add | solution.py:13
  405.0 6.5 %copy.17 = f32[2,8,128,512]{3,2,1,0:T(8,128)} copy(f32[2,8,128,512]{3,1,2,0:T(8,128)} %bitcast.63) | data formatting | bytes 8388608
  411.6 78.7 %all-reduce.1 = bf16[16,128,512]{2,1,0:T(8,128)(2,1)} all-reduce(f32[16,128,512]{2,1,0:T(8,128)} %bitcast.66), channel_id=1, replica_groups=mesh['groups'=2,'tm'=4,'chan'=4] {'chan'}, use_global_device_ids=true, to_apply=%region_6.7 | all-reduce | flops 1048576 | bytes 6291456 | tf_op jit(solution)/shard_map/psum | solution.py:69
  (41 shorter events, 39.8 us)
Async XLA Ops:
  0.0 29.8 %copy-start = (bf16[1,32,128,256]{3,2,1,0:T(8,128)(2,1)S(1)}, bf16[1,32,128,256]{3,2,1,0:T(8,128)(2,1)}, u32[]{:S(2)}) copy-start(bf16[1,32,128,256]{3,2,1,0:T(8,128)(2,1)} %param.10) | copy-start | bytes 6291460
  5.3 11.0 %all-to-all-start = ((s32[4,1,16]{2,1,0:T(1,128)}), s32[4,1,16]{2,1,0:T(1,128)S(1)}, u32[]{:S(2)}, u32[]{:S(2)}) async-start(s32[4,1,16]{2,1,0:T(1,128)} %bitcast.13), calls=%async_computation | async-start | bytes 4096 | tf_op jit(solution)/shard_map/all_to_all | solution.py:53
  16.3 9.0 %all-to-all-start.3 = ((bf16[4,16,2,128]{3,2,1,0:T(2,128)(2,1)}), bf16[4,16,2,128]{3,2,1,0:T(2,128)(2,1)S(1)}, u32[]{:S(2)}, u32[]{:S(2)}) async-start(bf16[4,16,2,128]{3,2,1,0:T(2,128)(2,1)} %broadcast_select_fusion.2), calls=%async_computation.3 | async-start | bytes 65536 | tf_op jit(solution)/shard_map/all_to_all | solution.py:51
  25.3 52.3 %all-to-all-start.2 = ((bf16[4,16,128,128]{3,2,1,0:T(8,128)(2,1)}), bf16[4,16,128,128]{3,2,1,0:T(8,128)(2,1)}, u32[]{:S(2)}, u32[]{:S(2)}) async-start(bf16[4,16,128,128]{3,2,1,0:T(8,128)(2,1)} %broadcast_select_fusion.1), calls=%async_computation.2 | async-start | bytes 4194304 | tf_op jit(solution)/shard_map/all_to_all | solution.py:50
  77.6 97.6 %all-to-all-start.1 = ((bf16[4,16,128,256]{2,3,1,0:T(8,128)(2,1)}), bf16[4,16,128,256]{2,3,1,0:T(8,128)(2,1)}, u32[]{:S(2)}, u32[]{:S(2)}) async-start(bf16[4,16,128,256]{2,3,1,0:T(8,128)(2,1)} %broadcast_select_fusion), calls=%async_computation.1 | async-start | bytes 8388608 | tf_op jit(solution)/shard_map/all_to_all | solution.py:52
  411.6 78.7 %copy-start.1 = (bf16[1,512,512]{2,1,0:T(8,128)(2,1)S(1)}, bf16[1,512,512]{2,1,0:T(8,128)(2,1)}, u32[]{:S(2)}) copy-start(bf16[1,512,512]{2,1,0:T(8,128)(2,1)} %param.13) | copy-start | bytes 1572868
where the time goes:
time: 495 us; the launch traced here: 493 us
  other arithmetic  169 us (34%)
  waiting for transfers between devices  128 us (26%)
  local copies, waits for them, and re-layouts  81.2 us (16%)
  blocking collectives  78.7 us (16%)
  starting transfers between devices  19.4 us (4%)
  matrix products  17.1 us (3%)
    scatter-add x4, other arithmetic, grid_group(): return total.at[targets].add(flat, mode='drop')  153 us
    all_to_all x1, waiting for transfers between devices, body(): lax.all_to_all(columns, 'tm', split_axis=0, concat_axis=0, tiled=True)  92.6 us
    psum x1, blocking collectives, body(): summed = lax.psum(partial_value, 'chan')  78.7 us
    all_to_all x1, waiting for transfers between devices, body(): lax.all_to_all(rows_sent, 'tm', split_axis=0, concat_axis=0, tiled=True)  34 us
    transpose x4, local copies, waits for them, and re-layouts, grid_group(): jnp.einsum('ghkv,gvq->gkhq', weighted, columns, preferred_element_type=jn...  28.8 us
    reshape x4, local copies, waits for them, and re-layouts, grid_group(): flat = patch.reshape(patch.shape[0], -1)  25.2 us
    dot_general x4, matrix products, grid_group(): jnp.einsum('ghkv,gvq->gkhq', weighted, columns, preferred_element_type=jn...  15.7 us
  transfers between devices with their start and end apart: 4, of which 3 were waited for; matrix products, arithmetic and copies ran while one was open for 5% of the time, Pallas kernels for 0%

commit v1 on v0

--- a/solution.py
+++ b/solution.py
@@ -5,6 +5,15 @@
 
 QW = 256
 GC = 4096
+
+
+def doubling_sum(block, mesh_axis):
+    devices = lax.axis_size(mesh_axis)
+    total, stride = (block, 1)
+    while stride < devices:
+        total = total + lax.ppermute(total, mesh_axis, [(i, i ^ stride) for i in range(devices)])
+        stride = 2 * stride
+    return total
 
 
 def grid_group(total, weighted, columns, targets):
@@ -66,7 +75,7 @@
     total, _ = lax.scan(step_raw, start, groups)
     partial_value = total.reshape(tile_count, rows_k, 2 * width_q)
     share = rows_k // lax.axis_size("chan")
-    summed = lax.psum(partial_value, "chan")
+    summed = doubling_sum(partial_value, "chan")
     mine = lax.dynamic_slice_in_dim(summed, lax.axis_index("chan") * share, share, 1)
     rounded = mine.astype(jnp.bfloat16)
     result = jnp.einsum("tkq,qr->ktr", rounded, w_kernel[0], preferred_element_type=jnp.float32)

time: 495 us -> 518 us (1.046)
  waiting for transfers between devices: 128 us -> 226 us
  blocking collectives: 78.7 us -> 0 us
    ppermute x0 -> x2, waiting for transfers between devices: none -> 98 us  [doubling_sum(): lax.ppermute(total, mesh_axis, [(i, i ^ stride) for i in range(devices)])]
    psum x1 -> x0, blocking collectives: 78.7 us -> none  [body(): summed = lax.psum(partial_value, 'chan')]
  transfers between devices with their start and end apart: 4 -> 6, of which waited for: 3 -> 5; matrix products, arithmetic and copies ran while one was open for 5% -> 4% of each run, Pallas kernels for 0% -> 0%
where the time goes in v1:
time: 518 us; the launch traced here: 515 us
  waiting for transfers between devices  226 us (44%)
  other arithmetic  170 us (33%)
  local copies, waits for them, and re-layouts  79.2 us (15%)
  starting transfers between devices  22.3 us (4%)
  matrix products  17.6 us (3%)
    scatter-add x4, other arithmetic, grid_group(): return total.at[targets].add(flat, mode='drop')  151 us
    ppermute x2, waiting for transfers between devices, doubling_sum(): lax.ppermute(total, mesh_axis, [(i, i ^ stride) for i in range(devices)])  98 us
    all_to_all x1, waiting for transfers between devices, body(): lax.all_to_all(columns, 'tm', split_axis=0, concat_axis=0, tiled=True)  92.6 us
    all_to_all x1, waiting for transfers between devices, body(): lax.all_to_all(rows_sent, 'tm', split_axis=0, concat_axis=0, tiled=True)  34 us
    transpose x4, local copies, waits for them, and re-layouts, grid_group(): jnp.einsum('ghkv,gvq->gkhq', weighted, columns, preferred_element_type=jn...  28.8 us
    reshape x4, local copies, waits for them, and re-layouts, grid_group(): flat = patch.reshape(patch.shape[0], -1)  25.2 us
    dot_general x4, matrix products, grid_group(): jnp.einsum('ghkv,gvq->gkhq', weighted, columns, preferred_element_type=jn...  15.7 us
  transfers between devices with their start and end apart: 6, of which 5 were waited for; matrix products, arithmetic and copies ran while one was open for 4% of the time, Pallas kernels for 0%

profile of v1, /device:TPU:1, one launch (start us, length us, event | category | flops | bytes accessed | tf_op | source)
XLA Modules:
  0.0 515.1 jit_solution(18330248097262054838)
XLA Ops:
  5.3 5.4 %all-to-all-start = ((s32[4,1,16]{2,1,0:T(1,128)}), s32[4,1,16]{2,1,0:T(1,128)S(1)}, u32[]{:S(2)}, u32[]{:S(2)}) async-start(s32[4,1,16]{2,1,0:T(1,128)} %bitcast.13), calls=%async_computation | async-start | bytes 4096 | tf_op jit(solution)/shard_map/all_to_all | solution.py:62
  16.2 4.5 all-to-all-start.3
  25.3 4.4 all-to-all-start.2
  32.5 6.4 %copy.14 = bf16[64,128,256]{1,2,0:T(8,128)(2,1)} copy(bf16[64,128,256]{2,1,0:T(8,128)(2,1)} %gather_fusion.1) | data formatting | bytes 8388608 | tf_op jit(solution)/shard_map/jit(_take)/gather | solution.py:54
  38.9 4.6 broadcast_select_fusion
  43.5 34.0 %all-to-all-done.2 = bf16[4,16,128,128]{3,2,1,0:T(8,128)(2,1)} async-done(((bf16[4,16,128,128]{3,2,1,0:T(8,128)(2,1)}), bf16[4,16,128,128]{3,2,1,0:T(8,128)(2,1)}, u32[]{:S(2)}, u32[]{:S(2)}) %all-to-all-start.2) | async-done | bytes 2097184 | tf_op jit(solution)/shard_map/all_to_all | solution.py:59
  77.5 5.0 all-to-all-start.1
  82.6 92.6 %all-to-all-done.1 = bf16[4,16,128,256]{2,3,1,0:T(8,128)(2,1)} async-done(((bf16[4,16,128,256]{2,3,1,0:T(8,128)(2,1)}), bf16[4,16,128,256]{2,3,1,0:T(8,128)(2,1)}, u32[]{:S(2)}, u32[]{:S(2)}) %all-to-all-start.1) | async-done | bytes 4194336 | tf_op jit(solution)/shard_map/all_to_all | solution.py:61
  177.4 225.7 %while.10 = (s32[]{:T(128)}, f32[16,65536]{1,0:T(8,128)}, s32[4,16]{1,0:T(4,128)S(1)}, bf16[4,16,128,256]{2,3,1,0:T(8,128)(2,1)}, bf16[4,16,128,128]{3,2,1,0:T(8...) while((s32[]{:T(128)}, f32[16,65536]{1,0:T(8,128)}, s32[4,16]{1,0:T(4,128)S(1)}, ...), condition=%wide.region_5.6_spmd, body=%wide.region_3.5_spmd.sunk | while | flops 270798912 | bytes 37266200 | solution.py:75
  182.4 7.2 %copy.19 = f32[16,128,2,256]{3,2,1,0:T(2,128)} copy(f32[16,128,2,256]{1,3,2,0:T(8,128)} %convolution_bitcast_fusion.3) | data formatting | bytes 8388608 | tf_op jit(solution)/shard_map/while/body/eval_jaxpr/ghkv,gvq->gkhq/transpose | solution.py:20
  189.6 6.3 %reshape.160 = f32[16,65536]{1,0:T(8,128)} reshape(f32[16,128,2,256]{3,2,1,0:T(2,128)} %copy.19) | data formatting | bytes 8388608 | tf_op jit(solution)/shard_map/while/body/eval_jaxpr/reshape | solution.py:21
  195.9 37.9 %scatter_fusion = f32[16,65536]{1,0:T(8,128)} fusion(f32[16,65536]{1,0:T(8,128)} %get-tuple-element.97, s32[16]{0:T(128)S(1)} %fusion.18, f32[16,65536]{1,0:T(8,128)} %reshape.160), kind=kCustom, calls=%fused_computation.4.clone.1 | custom fusion | flops 1048576 | bytes 12582976 | tf_op jit(solution)/shard_map/while/body/eval_jaxpr/scatter-add | solution.py:22
  238.9 7.2 %copy.19 = f32[16,128,2,256]{3,2,1,0:T(2,128)} copy(f32[16,128,2,256]{1,3,2,0:T(8,128)} %convolution_bitcast_fusion.3) | data formatting | bytes 8388608 | tf_op jit(solution)/shard_map/while/body/eval_jaxpr/ghkv,gvq->gkhq/transpose | solution.py:20
  246.1 6.3 %reshape.160 = f32[16,65536]{1,0:T(8,128)} reshape(f32[16,128,2,256]{3,2,1,0:T(2,128)} %copy.19) | data formatting | bytes 8388608 | tf_op jit(solution)/shard_map/while/body/eval_jaxpr/reshape | solution.py:21
  252.4 37.6 %scatter_fusion = f32[16,65536]{1,0:T(8,128)} fusion(f32[16,65536]{1,0:T(8,128)} %get-tuple-element.97, s32[16]{0:T(128)S(1)} %fusion.18, f32[16,65536]{1,0:T(8,128)} %reshape.160), kind=kCustom, calls=%fused_computation.4.clone.1 | custom fusion | flops 1048576 | bytes 12582976 | tf_op jit(solution)/shard_map/while/body/eval_jaxpr/scatter-add | solution.py:22
  295.1 7.2 %copy.19 = f32[16,128,2,256]{3,2,1,0:T(2,128)} copy(f32[16,128,2,256]{1,3,2,0:T(8,128)} %convolution_bitcast_fusion.3) | data formatting | bytes 8388608 | tf_op jit(solution)/shard_map/while/body/eval_jaxpr/ghkv,gvq->gkhq/transpose | solution.py:20
  302.3 6.3 %reshape.160 = f32[16,65536]{1,0:T(8,128)} reshape(f32[16,128,2,256]{3,2,1,0:T(2,128)} %copy.19) | data formatting | bytes 8388608 | tf_op jit(solution)/shard_map/while/body/eval_jaxpr/reshape | solution.py:21
  308.6 38.0 %scatter_fusion = f32[16,65536]{1,0:T(8,128)} fusion(f32[16,65536]{1,0:T(8,128)} %get-tuple-element.97, s32[16]{0:T(128)S(1)} %fusion.18, f32[16,65536]{1,0:T(8,128)} %reshape.160), kind=kCustom, calls=%fused_computation.4.clone.1 | custom fusion | flops 1048576 | bytes 12582976 | tf_op jit(solution)/shard_map/while/body/eval_jaxpr/scatter-add | solution.py:22
  351.7 7.2 %copy.19 = f32[16,128,2,256]{3,2,1,0:T(2,128)} copy(f32[16,128,2,256]{1,3,2,0:T(8,128)} %convolution_bitcast_fusion.3) | data formatting | bytes 8388608 | tf_op jit(solution)/shard_map/while/body/eval_jaxpr/ghkv,gvq->gkhq/transpose | solution.py:20
  358.9 6.3 %reshape.160 = f32[16,65536]{1,0:T(8,128)} reshape(f32[16,128,2,256]{3,2,1,0:T(2,128)} %copy.19) | data formatting | bytes 8388608 | tf_op jit(solution)/shard_map/while/body/eval_jaxpr/reshape | solution.py:21
  365.2 37.9 %scatter_fusion = f32[16,65536]{1,0:T(8,128)} fusion(f32[16,65536]{1,0:T(8,128)} %get-tuple-element.97, s32[16]{0:T(128)S(1)} %fusion.18, f32[16,65536]{1,0:T(8,128)} %reshape.160), kind=kCustom, calls=%fused_computation.4.clone.1 | custom fusion | flops 1048576 | bytes 12582976 | tf_op jit(solution)/shard_map/while/body/eval_jaxpr/scatter-add | solution.py:22
  403.1 4.6 copy.17
  409.7 6.8 %collective-permute-done = f32[16,128,512]{2,1,0:T(8,128)S(1)} collective-permute-done((f32[16,128,512]{2,1,0:T(8,128)S(1)}, f32[16,128,512]{2,1,0:T(8,128)S(1)}, u32[]{:S(2)}, u32[]{:S(2)}) %collective-permute-start) | collective-permute-done | bytes 4194336 | tf_op jit(solution)/shard_map/ppermute | solution.py:14
  420.3 91.2 %collective-permute-done.1 = f32[16,128,512]{2,1,0:T(8,128)} collective-permute-done((f32[16,128,512]{2,1,0:T(8,128)}, f32[16,128,512]{2,1,0:T(8,128)}, u32[]{:S(2)}, u32[]{:S(2)}) %collective-permute-start.1) | collective-permute-done | bytes 4194336 | tf_op jit(solution)/shard_map/ppermute | solution.py:14
  (45 shorter events, 50.0 us)
Async XLA Ops:
  0.0 29.7 %copy-start = (bf16[1,32,128,256]{3,2,1,0:T(8,128)(2,1)S(1)}, bf16[1,32,128,256]{3,2,1,0:T(8,128)(2,1)}, u32[]{:S(2)}) copy-start(bf16[1,32,128,256]{3,2,1,0:T(8,128)(2,1)} %param.10) | copy-start | bytes 6291460
  5.3 11.0 %all-to-all-start = ((s32[4,1,16]{2,1,0:T(1,128)}), s32[4,1,16]{2,1,0:T(1,128)S(1)}, u32[]{:S(2)}, u32[]{:S(2)}) async-start(s32[4,1,16]{2,1,0:T(1,128)} %bitcast.13), calls=%async_computation | async-start | bytes 4096 | tf_op jit(solution)/shard_map/all_to_all | solution.py:62
  16.2 9.0 %all-to-all-start.3 = ((bf16[4,16,2,128]{3,2,1,0:T(2,128)(2,1)}), bf16[4,16,2,128]{3,2,1,0:T(2,128)(2,1)S(1)}, u32[]{:S(2)}, u32[]{:S(2)}) async-start(bf16[4,16,2,128]{3,2,1,0:T(2,128)(2,1)} %broadcast_select_fusion.2), calls=%async_computation.3 | async-start | bytes 65536 | tf_op jit(solution)/shard_map/all_to_all | solution.py:60
  25.3 52.3 %all-to-all-start.2 = ((bf16[4,16,128,128]{3,2,1,0:T(8,128)(2,1)}), bf16[4,16,128,128]{3,2,1,0:T(8,128)(2,1)}, u32[]{:S(2)}, u32[]{:S(2)}) async-start(bf16[4,16,128,128]{3,2,1,0:T(8,128)(2,1)} %broadcast_select_fusion.1), calls=%async_computation.2 | async-start | bytes 4194304 | tf_op jit(solution)/shard_map/all_to_all | solution.py:59
  77.5 97.6 %all-to-all-start.1 = ((bf16[4,16,128,256]{2,3,1,0:T(8,128)(2,1)}), bf16[4,16,128,256]{2,3,1,0:T(8,128)(2,1)}, u32[]{:S(2)}, u32[]{:S(2)}) async-start(bf16[4,16,128,256]{2,3,1,0:T(8,128)(2,1)} %broadcast_select_fusion), calls=%async_computation.1 | async-start | bytes 8388608 | tf_op jit(solution)/shard_map/all_to_all | solution.py:61
  407.7 103.8 %copy-start.1 = (bf16[1,512,512]{2,1,0:T(8,128)(2,1)S(1)}, bf16[1,512,512]{2,1,0:T(8,128)(2,1)}, u32[]{:S(2)}) copy-start(bf16[1,512,512]{2,1,0:T(8,128)(2,1)} %param.13) | copy-start | bytes 1572868
  407.7 8.8 %collective-permute-start = (f32[16,128,512]{2,1,0:T(8,128)S(1)}, f32[16,128,512]{2,1,0:T(8,128)S(1)}, u32[]{:S(2)}, u32[]{:S(2)}) collective-permute-start(f32[16,128,512]{2,1,0:T(8,128)S(1)} %bitcast.66), channel_id=1, source_target_pairs={{0,1},{1,0},{2,3},{3,2},{4,5},{5,4},{6,7},{7,6},{8,9},{9,8},{10,11... | collective-permute-start | bytes 12582920 | tf_op jit(solution)/shard_map/ppermute | solution.py:14
  419.4 92.1 %collective-permute-start.1 = (f32[16,128,512]{2,1,0:T(8,128)}, f32[16,128,512]{2,1,0:T(8,128)}, u32[]{:S(2)}, u32[]{:S(2)}) collective-permute-start(f32[16,128,512]{2,1,0:T(8,128)} %bitcast_add_fusion.1), channel_id=1, source_target_pairs={{0,2},{1,3},{2,0},{3,1},{4,6},{5,7},{6,4},{7,5},{8,10},{9,11},{10,... | collective-permute-start | bytes 12582920 | tf_op jit(solution)/shard_map/ppermute | solution.py:14
